TPU v7x, 32 devices: a whole 2x2x4 slice. The times are simulated.
32 devices in a mesh: fsdp: 8 (over z, x), model: 4 (over y, core).
Axes of the slice: x: 2, y: 2, z: 4, core: 2. Of those that a mesh axis runs over, the one named last changes fastest.
Arguments:
- weight_query: bfloat16 [5120, 8192], P('fsdp', 'model'), may hold values from -0.125 to 0.125
- low_query: bfloat16 [5120, 32], P('fsdp'), may hold values from -0.078125 to 0.078125
- high_query: bfloat16 [32, 8192], P(None, 'model'), may hold values from -1 to 1
- weight_key: bfloat16 [5120, 1024], P('fsdp', 'model'), may hold values from -0.125 to 0.125
- low_key: bfloat16 [5120, 32], P('fsdp'), may hold values from -0.078125 to 0.078125
- high_key: bfloat16 [32, 1024], P(None, 'model'), may hold values from -1 to 1
- weight_value: bfloat16 [5120, 1024], P('fsdp', 'model'), may hold values from -0.125 to 0.125
- low_value: bfloat16 [5120, 32], P('fsdp'), may hold values from -0.078125 to 0.078125
- high_value: bfloat16 [32, 1024], P(None, 'model'), may hold values from -1 to 1
- norm_train: float32 [5120], P(('fsdp', 'model')), may hold values from 0.25 to 1.75
- norm_step: float32 [5120], P(('fsdp', 'model')), may hold values from -0.3 to 0.3
Outputs:
- final_query: bfloat16 [5120, 8192], P(None, 'model')
- final_key: bfloat16 [5120, 1024], P(None, 'model')
- final_value: bfloat16 [5120, 1024], P(None, 'model')
- column_query: float32 [8192], P('model')
- column_key: float32 [1024], P('model')
- column_value: float32 [1024], P('model')
- serve_norm: bfloat16 [5120], replicated
All inputs are finite; a program needn't handle non-finite values. Where the computation divides by a largest or mean magnitude, that divisor is 1e-20 or more.
Results may differ from a plain program's by a relative error of at most 0.001.
Values may be sent and summed in bfloat16 or wider, within the bound.
A program may use at most 128 MiB of HBM per device.

v0:
```python
import jax
import jax.numpy as jnp
from jax import lax
from jax.sharding import PartitionSpec as P

mix_rate = 0.5


def per_device(
    weight_query,
    low_query,
    high_query,
    weight_key,
    low_key,
    high_key,
    weight_value,
    low_value,
    high_value,
    norm_train,
    norm_step,
):
    result_query = weight_query.astype(jnp.float32) + mix_rate * jnp.dot(
        low_query, high_query, preferred_element_type=jnp.float32
    )
    result_key = weight_key.astype(jnp.float32) + mix_rate * jnp.dot(
        low_key, high_key, preferred_element_type=jnp.float32
    )
    result_value = weight_value.astype(jnp.float32) + mix_rate * jnp.dot(
        low_value, high_value, preferred_element_type=jnp.float32
    )
    column_query, column_key, column_value = lax.pmax(
        (
            jnp.max(jnp.abs(result_query), axis=0),
            jnp.max(jnp.abs(result_key), axis=0),
            jnp.max(jnp.abs(result_value), axis=0),
        ),
        "fsdp",
    )
    narrow_query, narrow_key, narrow_value = (
        (result_query / column_query).astype(jnp.bfloat16),
        (result_key / column_key).astype(jnp.bfloat16),
        (result_value / column_value).astype(jnp.bfloat16),
    )
    final_query, final_key, final_value = (
        lax.all_gather(narrow_query, "fsdp", axis=0, tiled=True),
        lax.all_gather(narrow_key, "fsdp", axis=0, tiled=True),
        lax.all_gather(narrow_value, "fsdp", axis=0, tiled=True),
    )
    serve_norm = lax.all_gather(
        (norm_train + norm_step).astype(jnp.bfloat16), ("fsdp", "model"), axis=0, tiled=True
    )
    return (final_query, final_key, final_value, column_query, column_key, column_value, serve_norm)


def solution(mesh):
    return jax.shard_map(
        per_device,
        mesh=mesh,
        in_specs=(
            P("fsdp", "model"),
            P("fsdp", None),
            P(None, "model"),
            P("fsdp", "model"),
            P("fsdp", None),
            P(None, "model"),
            P("fsdp", "model"),
            P("fsdp", None),
            P(None, "model"),
            P(("fsdp", "model")),
            P(("fsdp", "model")),
        ),
        out_specs=(
            P(None, "model"),
            P(None, "model"),
            P(None, "model"),
            P("model"),
            P("model"),
            P("model"),
            P(),
        ),
        check_vma=False,
    )
```

profile of v0, /device:TPU:0, one launch (start us, length us, event | category | flops | bytes accessed | tf_op | source)
XLA Modules:
  0.0 592.9 jit_solution(10211061483440322897)
XLA Ops:
  7.2 0.0 copy-start
  7.2 0.0 all-gather.6.cloned.1.call-start
  7.2 1.3 abs_reduce_fusion.2
  8.6 1.3 abs_reduce_fusion.1
  9.9 0.0 copy-done
  9.9 5.0 abs_reduce_fusion
  14.9 38.8 %all-reduce.1 = (f32[2048]{0:T(1024)S(1)}, f32[256]{0:T(256)S(1)}, f32[256]{0:T(256)S(1)}) all-reduce(f32[2048]{0:T(1024)S(1)} %get-tuple-element.10, f32[256]{0:T(256)S(1)} %get-tuple-element.12, f32[256]{0:T(256)S(1)} %get-tuple-element.14), channel_id=1, replica_groups=mesh['fsdp'=8,'model'=4] {'fsdp'}, use_global_device_ids=true, to_apply=%region_1.0 | all-reduce | flops 2560 | bytes 20480 | tf_op jit(solution)/shard_map/pmax | solution.py:31
  53.7 0.0 copy-start.3
  53.7 0.0 copy-start.4
  53.7 0.0 copy-start.5
  53.7 0.8 divide_convert_fusion.2
  54.5 0.0 all-gather.6.cloned.1.call-update
  54.5 0.0 all-gather.8.cloned.1.call-start
  54.6 0.8 divide_convert_fusion.1
  55.3 0.0 all-gather.8.cloned.1.call-update
  55.4 0.0 all-gather.4.cloned.1.call-start
  55.4 0.0 copy-start.6
  55.4 0.0 copy-start.7
  55.4 4.7 divide_convert_fusion
  60.1 0.0 copy-done.3
  60.1 0.0 copy-done.4
  60.1 0.0 copy-done.5
  60.1 0.0 all-gather.4.cloned.1.call-update
  60.1 0.0 copy-done.6
  60.1 0.0 copy-done.7
  60.2 0.2 dynamic-update-slice
  60.4 38.8 %all-reduce = bf16[5120]{0:T(1024)(128)(2,1)} all-reduce(bf16[5120]{0:T(1024)(128)(2,1)S(1)} %dynamic-update-slice), channel_id=1, replica_groups=mesh['fsdp'=8,'model'=4] {'fsdp','model'}, use_global_device_ids=true, to_apply=%add | all-reduce | flops 5120 | bytes 20480
  99.2 7.6 %all-gather.6.cloned.1.call-done = bf16[5120,256]{1,0:T(8,128)(2,1)} async-done(((bf16[640,256]{1,0:T(8,128)(2,1)}), bf16[5120,256]{1,0:T(8,128)(2,1)}) %all-gather.6.cloned.1.call-update) | async-done | bytes 2621456 | tf_op jit(solution)/shard_map/all_gather | solution.py:46
  106.9 0.0 copy-start.1
  106.9 55.3 %all-gather.8.cloned.1.call-done = bf16[5120,256]{1,0:T(8,128)(2,1)} async-done(((bf16[640,256]{1,0:T(8,128)(2,1)}), bf16[5120,256]{1,0:T(8,128)(2,1)}) %all-gather.8.cloned.1.call-update) | async-done | bytes 2621456 | tf_op jit(solution)/shard_map/all_gather | solution.py:47
  162.2 402.4 %all-gather.4.cloned.1.call-done = bf16[5120,2048]{1,0:T(8,128)(2,1)} async-done(((bf16[640,2048]{1,0:T(8,128)(2,1)}), bf16[5120,2048]{1,0:T(8,128)(2,1)}) %all-gather.4.cloned.1.call-update) | async-done | bytes 20971536 | tf_op jit(solution)/shard_map/all_gather | solution.py:45
  564.6 17.6 %copy.22 = bf16[5120,2048]{1,0:T(8,128)(2,1)} copy(bf16[5120,2048]{1,0:T(8,128)(2,1)} %all-gather.4.cloned.1.call-done) | data formatting | bytes 41943040
  582.2 0.0 copy-done.1
  582.2 0.0 copy-start.2
  582.2 1.5 copy.23
  583.7 1.2 copy-done.2
  584.9 1.5 copy.24
  (2 shorter events, 0.0 us)
Async XLA Ops:
  7.2 2.7 copy-start
  7.2 99.7 %all-gather.6.cloned.1.call-start = ((), (), s32[]{:S(2)}) async-start(), calls=%async_computation.1 | async-start | bytes 2949120 | tf_op jit(solution)/shard_map/all_gather | solution.py:46
  53.7 6.4 %copy-start.3 = (f32[2048]{0:T(1024)}, f32[2048]{0:T(1024)S(1)}, u32[]{:S(2)}) copy-start(f32[2048]{0:T(1024)S(1)} %get-tuple-element.26) | copy-start | bytes 24580
  53.7 6.4 %copy-start.4 = (f32[256]{0:T(256)}, f32[256]{0:T(256)S(1)}, u32[]{:S(2)}) copy-start(f32[256]{0:T(256)S(1)} %get-tuple-element.27) | copy-start | bytes 3076
  53.7 6.4 %copy-start.5 = (f32[256]{0:T(256)}, f32[256]{0:T(256)S(1)}, u32[]{:S(2)}) copy-start(f32[256]{0:T(256)S(1)} %get-tuple-element.28) | copy-start | bytes 3076
  54.5 107.7 %all-gather.8.cloned.1.call-start = ((), (), s32[]{:S(2)}) async-start(), calls=%async_computation.2 | async-start | bytes 2949120 | tf_op jit(solution)/shard_map/all_gather | solution.py:47
  55.4 509.3 %all-gather.4.cloned.1.call-start = ((), (), s32[]{:S(2)}) async-start(), calls=%async_computation | async-start | bytes 23592960 | tf_op jit(solution)/shard_map/all_gather | solution.py:45
  55.4 4.7 copy-start.6
  55.4 4.7 copy-start.7
  106.9 475.4 %copy-start.1 = (bf16[5120,256]{1,0:T(8,128)(2,1)S(1)}, bf16[5120,256]{1,0:T(8,128)(2,1)}, u32[]{:S(2)}) copy-start(bf16[5120,256]{1,0:T(8,128)(2,1)} %all-gather.6.cloned.1.call-done) | copy-start | bytes 7864324
  582.2 2.7 copy-start.2
Sparse Core Ops, SparseCore 0:
  54.6 52.1 all-gather.5
  109.1 53.0 all-gather.7
  164.3 400.2 all-gather.3
where the time goes:
time: 593 us
  waiting for transfers between devices  465 us (78%)
  blocking collectives  77.6 us (13%)
  local copies, waits for them, and re-layouts  22.1 us (4%)
  between operations  13.8 us (2%)
  matrix products  7.65 us (1%)
  other arithmetic  6.2 us (1%)
    all_gather x1, waiting for transfers between devices, per_device(): lax.all_gather(narrow_query, 'fsdp', axis=0, tiled=True)  402 us
    all_gather x1, waiting for transfers between devices, per_device(): lax.all_gather(narrow_value, 'fsdp', axis=0, tiled=True)  55.3 us
    pmax x1, blocking collectives, per_device(): lax.pmax((jnp.max(jnp.abs(result_query), axis=0), jnp.max(jnp.abs(result_...  38.8 us
    unnamed x1, blocking collectives  38.8 us
    unnamed x21, local copies, waits for them, and re-layouts  22.1 us
  transfers between devices with their start and end apart: 3, of which 3 were waited for; matrix products, arithmetic and copies ran while one was open for 1% of the time, Pallas kernels for 0%

commit v1 on v0

v1 whole, which is shorter than its diff:
```python
import functools

import jax
import jax.numpy as jnp
from jax import lax
from jax.experimental import pallas as pl
from jax.experimental.pallas import tpu as pltpu
from jax.sharding import PartitionSpec as P

mix_rate = 0.5
MESH = pl.DeviceIdType.MESH
QUERY_PIECES = 4


def split_rows(rows, parts):
    tiles = rows // 16
    parts = min(parts, tiles)
    edges = [16 * (tiles * i // parts) for i in range(parts + 1)]
    return [(a, b - a) for a, b in zip(edges, edges[1:])]


def merge_gather(n, wq, wk, wv, lq, lk, lv, hq, hk, hv, fq, fk, fv, cq, ck, cv,
                 rq, rk, rv, maxes, max_send, max_recv, send_sem, recv_sem):
    me = lax.axis_index("fsdp")
    half = n // 2

    def at(p):
        p = lax.rem(p + 2 * n, n)
        side = p // half
        z = p + side * (n - 1 - 2 * p)
        return z * 2 + side

    z, x = me // 2, lax.rem(me, 2)
    pos = z + x * (n - 1 - 2 * z)

    barrier = pltpu.get_barrier_semaphore()
    for d in range(1, n):
        pl.semaphore_signal(barrier, inc=1, device_id={"fsdp": lax.rem(me + d, n)}, device_id_type=MESH)

    rows = wq.shape[0]
    step_rows = 64 if rows % 64 == 0 else rows
    groups = ((wq, lq, hq, rq, cq, fq), (wk, lk, hk, rk, ck, fk), (wv, lv, hv, rv, cv, fv))
    start = 0
    spans = []
    for w, low, high, res, _, _ in groups:
        width = w.shape[1]
        tile = min(width, 512)
        for c in range(0, width, tile):
            cols = slice(c, c + tile)
            delta = lax.dot_general(low[...], high[:, cols], (((0,), (0,)), ((), ())),
                                    preferred_element_type=jnp.float32)
            out = w[:, cols].astype(jnp.float32) + mix_rate * delta
            res[:, cols] = out
            maxes[me, :, start + c:start + c + tile] = jnp.max(jnp.abs(out), axis=0, keepdims=True)
        spans.append((start, width))
        start += width

    pl.semaphore_wait(barrier, n - 1)
    copies = []
    for d in range(1, n):
        copy = pltpu.make_async_remote_copy(
            src_ref=maxes.at[me], dst_ref=maxes.at[me],
            send_sem=max_send.at[d], recv_sem=max_recv.at[d],
            device_id={"fsdp": lax.rem(me + d, n)}, device_id_type=MESH)
        copy.start()
        copies.append(copy)
    for copy in copies:
        copy.wait()

    base = pl.multiple_of(me * rows, rows)
    for (s, width), (_, _, _, res, col, fin) in zip(spans, groups):
        top = jnp.max(maxes[:, 0, s:s + width], axis=0, keepdims=True)
        col[...] = top

        @pl.loop(0, rows // step_rows)
        def _(i):
            r = pl.multiple_of(i * step_rows, step_rows)
            fin[pl.ds(base + r, step_rows), :] = (res[pl.ds(r, step_rows), :] / top).astype(jnp.bfloat16)

    h = rows // 2
    pieces = [(fq, a, b) for a, b in split_rows(h, QUERY_PIECES)] + [(fk, 0, h), (fv, 0, h)]
    count = len(pieces)

    def piece_copy(step, which, k):
        ref, a, size = pieces[k]
        sign = 1 - 2 * which
        owner = at(pos - sign * step)
        window = ref.at[pl.ds(pl.multiple_of(owner * rows + which * h + a, 16), size)]
        i = (step * 2 + which) * count + k
        return pltpu.make_async_remote_copy(
            src_ref=window, dst_ref=window, send_sem=send_sem.at[i], recv_sem=recv_sem.at[i],
            device_id={"fsdp": at(pos + sign)}, device_id_type=MESH)

    def arrival(step, which, k):
        ref, a, size = pieces[k]
        sign = 1 - 2 * which
        owner = at(pos - sign * (step + 1))
        window = ref.at[pl.ds(pl.multiple_of(owner * rows + which * h + a, 16), size)]
        i = (step * 2 + which) * count + k
        pltpu.make_async_remote_copy(
            src_ref=window, dst_ref=window, send_sem=send_sem.at[i], recv_sem=recv_sem.at[i],
            device_id={"fsdp": at(pos + sign)}, device_id_type=MESH).wait_recv()

    for k in range(count):
        for which in range(2):
            piece_copy(0, which, k).start()

    @pl.loop(1, n - 1)
    def _(step):
        for k in range(count):
            for which in range(2):
                arrival(step - 1, which, k)
                piece_copy(step, which, k).start()

    for k in range(count):
        for which in range(2):
            arrival(n - 2, which, k)

    @pl.loop(0, n - 1)
    def _(step):
        for k in range(count):
            for which in range(2):
                piece_copy(step, which, k).wait_send()


def solution(mesh):
    n = mesh.shape["fsdp"]

    def per_device(wq, lq, hq, wk, lk, hk, wv, lv, hv, norm_train, norm_step):
        rows = wq.shape[0]
        widths = [w.shape[1] for w in (wq, wk, wv)]
        count = len(split_rows(rows // 2, QUERY_PIECES)) + 2
        vmem = pl.BlockSpec(memory_space=pltpu.VMEM)
        fq, fk, fv, cq, ck, cv = pl.pallas_call(
            functools.partial(merge_gather, n),
            out_shape=[pltpu.VMEM((n * rows, w), jnp.bfloat16) for w in widths]
            + [jax.ShapeDtypeStruct((1, w), jnp.float32) for w in widths],
            in_specs=[vmem] * 9,
            out_specs=[vmem] * 6,
            scratch_shapes=[pltpu.VMEM((rows, w), jnp.float32) for w in widths]
            + [
                pltpu.VMEM((n, 1, sum(widths)), jnp.float32),
                pltpu.SemaphoreType.DMA((n,)),
                pltpu.SemaphoreType.DMA((n,)),
                pltpu.SemaphoreType.DMA(((n - 1) * 2 * count,)),
                pltpu.SemaphoreType.DMA(((n - 1) * 2 * count,)),
            ],
            compiler_params=pltpu.CompilerParams(
                collective_id=0, has_side_effects=True, vmem_limit_bytes=24 * 1024 * 1024),
        )(wq, wk, wv, lq.T, lk.T, lv.T, hq, hk, hv)
        serve_norm = lax.all_gather(
            (norm_train + norm_step).astype(jnp.bfloat16), ("fsdp", "model"), axis=0, tiled=True)
        return (fq, fk, fv, cq.reshape(-1), ck.reshape(-1), cv.reshape(-1), serve_norm)

    return jax.shard_map(
        per_device,
        mesh=mesh,
        in_specs=(
            P("fsdp", "model"), P("fsdp", None), P(None, "model"),
            P("fsdp", "model"), P("fsdp", None), P(None, "model"),
            P("fsdp", "model"), P("fsdp", None), P(None, "model"),
            P(("fsdp", "model")), P(("fsdp", "model")),
        ),
        out_specs=(P(None, "model"), P(None, "model"), P(None, "model"),
                   P("model"), P("model"), P("model"), P()),
        check_vma=False,
    )
```

time: 593 us -> 320 us (0.54)
  waiting for transfers between devices: 465 us -> 0 us
  Pallas kernels: 0 us -> 258 us
  blocking collectives: 77.6 us -> 40.2 us
  between operations: 13.8 us -> 0.68 us
  matrix products: 7.65 us -> 0 us
  other arithmetic: 6.2 us -> 0.01 us
    all_gather x3 -> x0, waiting for transfers between devices: 465 us -> none  [the longest x1 402 us: per_device(): lax.all_gather(narrow_query, 'fsdp', axis=0, tiled=True)]
    pallas_call x0 -> x1, Pallas kernels: none -> 258 us  [per_device(): pl.pallas_call(functools.partial(merge_gather, n), out_shape=[pltpu.VMEM(...]
    pmax x1 -> x0, blocking collectives: 38.8 us -> none  [per_device(): lax.pmax((jnp.max(jnp.abs(result_query), axis=0), jnp.max(jnp.abs(result_...]
    dot_general x3 -> x0, matrix products: 7.65 us -> none  [the longest x1 5 us: per_device(): jnp.dot(low_query, high_query, preferred_element_type=jnp.float32)]
    convert_element_type x3 -> x0, other arithmetic: 6.2 us -> none  [the longest x1 4.65 us: per_device(): (result_query / column_query).astype(jnp.bfloat16)]
    unnamed x21 -> x30, local copies, waits for them, and re-layouts: 22.1 us -> 20.9 us
  transfers between devices with their start and end apart: 3 -> 0, of which waited for: 3 -> 0; matrix products, arithmetic and copies ran while one was open for 1% -> 0% of each run, Pallas kernels for 0% -> 0%
where the time goes in v1:
time: 320 us
  Pallas kernels  258 us (81%)
  blocking collectives  40.2 us (13%)
  local copies, waits for them, and re-layouts  20.9 us (7%)
    pallas_call x1, Pallas kernels, per_device(): pl.pallas_call(functools.partial(merge_gather, n), out_shape=[pltpu.VMEM(...  258 us
    unnamed x1, blocking collectives  40.2 us
    unnamed x30, local copies, waits for them, and re-layouts  20.9 us

profile of v1, /device:TPU:0, one launch (start us, length us, event | category | flops | bytes accessed | tf_op | source)
XLA Modules:
  0.0 319.9 jit_solution(13438939375134942402)
XLA Ops:
  0.6 0.0 copy-start
  0.6 1.7 copy-done
  2.4 0.0 copy-start.1
  2.4 1.0 copy-done.1
  3.4 0.0 copy-start.2
  3.4 1.0 copy-done.2
  4.3 0.0 copy-start.3
  4.3 0.9 copy-done.3
  5.2 0.0 copy-start.4
  5.2 0.8 copy-done.4
  6.0 0.0 copy-start.5
  6.0 0.8 copy-done.5
  6.8 0.0 copy-start.6
  6.8 0.8 copy-done.6
  7.6 0.0 copy-start.7
  7.6 0.7 copy-done.7
  8.3 0.0 copy-start.8
  8.3 0.7 copy-done.8
  9.0 258.1 %shard_map.162 = (bf16[5120,2048]{1,0:T(8,128)(2,1)S(1)}, bf16[5120,256]{1,0:T(8,128)(2,1)S(1)}, bf16[5120,256]{1,0:T(8,128)(2,1)S(1)}, f32[1,2048]{1,0:T(1,128)...) custom-call(bf16[640,2048]{1,0:T(8,128)(2,1)S(1)} %copy-done, bf16[640,256]{1,0:T(8,128)(2,1)S(1)} %copy-done.1, ...), custom_call_target="tpu_custom_call" | custom-call | tf_op jit(solution)/shard_map/pallas_call | solution.py:134
  267.1 7.5 %copy.25 = bf16[5120,2048]{1,0:T(8,128)(2,1)} copy(bf16[5120,2048]{1,0:T(8,128)(2,1)S(1)} %get-tuple-element.19) | data formatting | bytes 41943040
  274.6 1.5 copy.26
  276.1 0.0 copy-start.9
  276.1 0.0 copy-start.10
  276.1 1.5 copy.27
  277.6 0.0 copy-done.9
  277.6 0.0 copy-done.10
  277.6 0.2 dynamic-update-slice
  277.9 40.2 %all-reduce = bf16[5120]{0:T(1024)(128)(2,1)} all-reduce(bf16[5120]{0:T(1024)(128)(2,1)S(1)} %dynamic-update-slice), channel_id=1, replica_groups=mesh['fsdp'=8,'model'=4] {'fsdp','model'}, use_global_device_ids=true, to_apply=%add | all-reduce | flops 5120 | bytes 20480
  318.1 0.6 copy.28
  318.7 0.6 copy.29
  319.3 0.6 copy.30
  (2 shorter events, 0.0 us)
Async XLA Ops:
  0.6 1.7 copy-start
  2.4 1.0 copy-start.1
  3.4 1.0 copy-start.2
  4.3 0.9 copy-start.3
  5.2 0.8 copy-start.4
  6.0 0.8 copy-start.5
  6.8 0.8 copy-start.6
  7.6 0.7 copy-start.7
  8.3 0.7 copy-start.8
  276.1 1.5 copy-start.9
  276.1 1.5 copy-start.10

commit v2 on v1

--- a/solution.py
+++ b/solution.py
@@ -19,9 +19,12 @@
     return [(a, b - a) for a, b in zip(edges, edges[1:])]
 
 
-def merge_gather(n, wq, wk, wv, lq, lk, lv, hq, hk, hv, fq, fk, fv, cq, ck, cv,
-                 rq, rk, rv, maxes, max_send, max_recv, send_sem, recv_sem):
+def merge_gather(n, m, hwq, hwk, hwv, hlq, hlk, hlv, hhq, hhk, hhv, htrain, hstep,
+                 fq, fk, fv, cq, ck, cv, gains,
+                 wq, wk, wv, lq, lk, lv, hq, hk, hv, train, step_gain, own_gain,
+                 rq, rk, rv, maxes, load_sem, max_send, max_recv, gain_send, gain_recv, send_sem, recv_sem):
     me = lax.axis_index("fsdp")
+    lane = lax.axis_index("model")
     half = n // 2
 
     def at(p):
@@ -33,16 +36,29 @@
     z, x = me // 2, lax.rem(me, 2)
     pos = z + x * (n - 1 - 2 * z)
 
+    staged = ((hwk, wk), (hlk, lk), (hhk, hk), (hwv, wv), (hlv, lv), (hhv, hv),
+              (hwq, wq), (hlq, lq), (hhq, hq), (htrain, train), (hstep, step_gain))
+    loads = [pltpu.make_async_copy(src, dst, load_sem.at[i]) for i, (src, dst) in enumerate(staged)]
+    for load in loads:
+        load.start()
+
     barrier = pltpu.get_barrier_semaphore()
-    for d in range(1, n):
-        pl.semaphore_signal(barrier, inc=1, device_id={"fsdp": lax.rem(me + d, n)}, device_id_type=MESH)
+    others = [(d, e) for d in range(n) for e in range(m) if d or e]
+
+    def peer(d, e):
+        return {"fsdp": lax.rem(me + d, n), "model": lax.rem(lane + e, m)}
+
+    for d, e in others:
+        pl.semaphore_signal(barrier, inc=1, device_id=peer(d, e), device_id_type=MESH)
 
     rows = wq.shape[0]
     step_rows = 64 if rows % 64 == 0 else rows
-    groups = ((wq, lq, hq, rq, cq, fq), (wk, lk, hk, rk, ck, fk), (wv, lv, hv, rv, cv, fv))
+    groups = ((wk, lk, hk, rk, ck, fk), (wv, lv, hv, rv, cv, fv), (wq, lq, hq, rq, cq, fq))
     start = 0
     spans = []
-    for w, low, high, res, _, _ in groups:
+    for g, (w, low, high, res, _, _) in enumerate(groups):
+        for load in loads[3 * g:3 * g + 3]:
+            load.wait()
         width = w.shape[1]
         tile = min(width, 512)
         for c in range(0, width, tile):
@@ -54,14 +70,17 @@
             maxes[me, :, start + c:start + c + tile] = jnp.max(jnp.abs(out), axis=0, keepdims=True)
         spans.append((start, width))
         start += width
-
-    pl.semaphore_wait(barrier, n - 1)
+    for load in loads[9:]:
+        load.wait()
+    own_gain[...] = train[...] + step_gain[...]
+
+    pl.semaphore_wait(barrier, len(others))
     copies = []
     for d in range(1, n):
         copy = pltpu.make_async_remote_copy(
             src_ref=maxes.at[me], dst_ref=maxes.at[me],
             send_sem=max_send.at[d], recv_sem=max_recv.at[d],
-            device_id={"fsdp": lax.rem(me + d, n)}, device_id_type=MESH)
+            device_id=peer(d, 0), device_id_type=MESH)
         copy.start()
         copies.append(copy)
     for copy in copies:
@@ -105,6 +124,18 @@
         for which in range(2):
             piece_copy(0, which, k).start()
 
+    gain_copies = []
+    for i, (d, e) in enumerate(others):
+        copy = pltpu.make_async_remote_copy(
+            src_ref=own_gain, dst_ref=gains.at[me * m + lane],
+            send_sem=gain_send.at[i], recv_sem=gain_recv.at[i],
+            device_id=peer(d, e), device_id_type=MESH)
+        copy.start()
+        gain_copies.append(copy)
+    gains[me * m + lane] = own_gain[...]
+    for copy in gain_copies:
+        copy.wait()
+
     @pl.loop(1, n - 1)
     def _(step):
         for k in range(count):
@@ -123,33 +154,65 @@
                 piece_copy(step, which, k).wait_send()
 
 
+def write_out(sizes, *refs):
+    count = len(sizes)
+    srcs, dsts, sem = refs[:count], refs[count:2 * count], refs[2 * count]
+    copies = []
+    for src, dst, parts in zip(srcs, dsts, sizes):
+        size = src.shape[0] // parts
+        for p in range(parts):
+            window = pl.ds(p * size, size)
+            copies.append(pltpu.make_async_copy(src.at[window], dst.at[window], sem.at[len(copies)]))
+    for copy in copies:
+        copy.start()
+    for copy in copies:
+        copy.wait()
+
+
 def solution(mesh):
-    n = mesh.shape["fsdp"]
+    n, m = mesh.shape["fsdp"], mesh.shape["model"]
 
     def per_device(wq, lq, hq, wk, lk, hk, wv, lv, hv, norm_train, norm_step):
         rows = wq.shape[0]
         widths = [w.shape[1] for w in (wq, wk, wv)]
         count = len(split_rows(rows // 2, QUERY_PIECES)) + 2
+        own = norm_train.shape[0]
+        hbm = pl.BlockSpec(memory_space=pltpu.HBM)
         vmem = pl.BlockSpec(memory_space=pltpu.VMEM)
-        fq, fk, fv, cq, ck, cv = pl.pallas_call(
-            functools.partial(merge_gather, n),
+        args = (wq, wk, wv, lq.T, lk.T, lv.T, hq, hk, hv, norm_train.reshape(1, own), norm_step.reshape(1, own))
+        *held, gains = pl.pallas_call(
+            functools.partial(merge_gather, n, m),
             out_shape=[pltpu.VMEM((n * rows, w), jnp.bfloat16) for w in widths]
-            + [jax.ShapeDtypeStruct((1, w), jnp.float32) for w in widths],
-            in_specs=[vmem] * 9,
-            out_specs=[vmem] * 6,
-            scratch_shapes=[pltpu.VMEM((rows, w), jnp.float32) for w in widths]
+            + [pltpu.VMEM((1, w), jnp.float32) for w in widths]
+            + [pltpu.VMEM((n * m, 1, own), jnp.float32)],
+            in_specs=[hbm] * len(args),
+            out_specs=[vmem] * 7,
+            scratch_shapes=[pltpu.VMEM(a.shape, a.dtype) for a in args]
+            + [pltpu.VMEM((1, own), jnp.float32)]
+            + [pltpu.VMEM((rows, w), jnp.float32) for w in widths]
             + [
                 pltpu.VMEM((n, 1, sum(widths)), jnp.float32),
+                pltpu.SemaphoreType.DMA((len(args),)),
                 pltpu.SemaphoreType.DMA((n,)),
                 pltpu.SemaphoreType.DMA((n,)),
+                pltpu.SemaphoreType.DMA((n * m,)),
+                pltpu.SemaphoreType.DMA((n * m,)),
                 pltpu.SemaphoreType.DMA(((n - 1) * 2 * count,)),
                 pltpu.SemaphoreType.DMA(((n - 1) * 2 * count,)),
             ],
             compiler_params=pltpu.CompilerParams(
-                collective_id=0, has_side_effects=True, vmem_limit_bytes=24 * 1024 * 1024),
-        )(wq, wk, wv, lq.T, lk.T, lv.T, hq, hk, hv)
-        serve_norm = lax.all_gather(
-            (norm_train + norm_step).astype(jnp.bfloat16), ("fsdp", "model"), axis=0, tiled=True)
+                collective_id=0, has_side_effects=True, vmem_limit_bytes=67043328 - 2 * n * rows * sum(widths) - 4 * 8 * sum(widths) - 32768 * 4 - 1048576),
+        )(*args)
+        sizes = (8, 2, 2, 1, 1, 1)
+        fq, fk, fv, cq, ck, cv = pl.pallas_call(
+            functools.partial(write_out, sizes),
+            out_shape=[jax.ShapeDtypeStruct(a.shape, a.dtype) for a in held],
+            in_specs=[vmem] * 6,
+            out_specs=[hbm] * 6,
+            scratch_shapes=[pltpu.SemaphoreType.DMA((sum(sizes),))],
+            compiler_params=pltpu.CompilerParams(vmem_limit_bytes=1024 * 1024),
+        )(*held)
+        serve_norm = gains.reshape(-1).astype(jnp.bfloat16)
         return (fq, fk, fv, cq.reshape(-1), ck.reshape(-1), cv.reshape(-1), serve_norm)
 
     return jax.shard_map(

time: 320 us -> 275 us (0.86)
  blocking collectives: 40.2 us -> 0 us
  local copies, waits for them, and re-layouts: 20.9 us -> 0.7 us
  Pallas kernels: 258 us -> 274 us
    unnamed x1 -> x0, blocking collectives: 40.2 us -> none
    unnamed x30 -> x0, local copies, waits for them, and re-layouts: 20.9 us -> none
    pallas_call x1 -> x2, Pallas kernels: 258 us -> 274 us  [the longest x1 265 us: per_device(): pl.pallas_call(functools.partial(merge_gather, n, m), out_shape=[pltpu.VM...]
where the time goes in v2:
time: 275 us
  Pallas kernels  274 us (100%)
    pallas_call x1, Pallas kernels, per_device(): pl.pallas_call(functools.partial(merge_gather, n, m), out_shape=[pltpu.VM...  265 us
    pallas_call x1, Pallas kernels, per_device(): pl.pallas_call(functools.partial(write_out, sizes), out_shape=[jax.ShapeD...  8.83 us

profile of v2, /device:TPU:0, one launch (start us, length us, event | category | flops | bytes accessed | tf_op | source)
XLA Modules:
  0.0 275.3 jit_solution(4206488711391898221)
XLA Ops:
  0.6 265.0 %shard_map.162 = (bf16[5120,2048]{1,0:T(8,128)(2,1)S(1)}, bf16[5120,256]{1,0:T(8,128)(2,1)S(1)}, bf16[5120,256]{1,0:T(8,128)(2,1)S(1)}, f32[1,2048]{1,0:T(1,128)...) custom-call(bf16[640,2048]{1,0:T(8,128)(2,1)} %hwq.1, bf16[640,256]{1,0:T(8,128)(2,1)} %hwk.1, ...), custom_call_target="tpu_custom_call" | custom-call | tf_op jit(solution)/shard_map/pallas_call | solution.py:183
  265.7 8.8 %shard_map.163 = (bf16[5120,2048]{1,0:T(8,128)(2,1)}, bf16[5120,256]{1,0:T(8,128)(2,1)}, bf16[5120,256]{1,0:T(8,128)(2,1)}, f32[1,2048]{1,0:T(1,128)}, f32[1,256]{1,0:T(1,128)}, /*index=5*/f32[1,256]{1,0:T(1,128)}) custom-call(bf16[5120,2048]{1,0:T(8,128)(2,1)S(1)} %get-tuple-element.20.refs_0_, bf16[5120,256]{1,0:T(8,128)(2,1)S(1)} %get-tuple-element.21.refs_1_, ...), custom_call_target="tpu_custom_call" | custom-call | tf_op jit(solution)/shard_map/pallas_call | solution.py:207
  274.5 0.1 convert_reduce_fusion
  274.6 0.7 convert_element_type.7
